TPU v7x, 8 devices: a whole 2x2x1 slice. The times are simulated.
8 devices in a mesh: batch: 1 (over z), cx: 2 (over y), cy: 4 (over x, core).
Axes of the slice: x: 2, y: 2, z: 1, core: 2. Of those that a mesh axis runs over, the one named last changes fastest.
Arguments:
- q_tok: bfloat16 [1024, 40, 128], P(('batch', 'cx', 'cy'))
- k_tok: bfloat16 [1024, 8, 128], P(('batch', 'cx', 'cy'))
- v_tok: bfloat16 [1024, 8, 128], P(('batch', 'cx', 'cy'))
Outputs:
- output: bfloat16 [1024, 40, 128], P(('batch', 'cx', 'cy'))
All inputs are finite; a program needn't handle non-finite values.
Results may differ from a plain program's by a relative error of at most 0.00437211.
Values are sent between devices in bfloat16 or wider.
A program may use at most 1 GiB of HBM per device.

v0:
```python
import jax
import jax.numpy as jnp
from jax import lax
from jax.sharding import PartitionSpec as P

CTX_AXES = ("cx", "cy")


def solution(mesh):
    size_cy = mesh.shape["cy"]
    num_ranks = mesh.shape["cx"] * size_cy
    next_rank = [(source, (source + 1) % num_ranks) for source in range(num_ranks)]
    seq_spec = P(("batch", "cx", "cy"), None, None)

    def local_attend(q_loc, k_loc, v_loc):
        tokens, num_heads, head_dim = q_loc.shape
        num_kv = k_loc.shape[1]
        group_size = num_heads // num_kv
        q_grp = q_loc.reshape(tokens, num_kv, group_size, head_dim)
        q_scale = head_dim ** -0.5
        my_rank = lax.axis_index("cx") * size_cy + lax.axis_index("cy")
        positions = jnp.arange(tokens)
        diag_keep = positions[:, None, None] >= positions[None, None, :]

        def absorb(running, kv_blk, keep_mask):
            run_max, run_sum, out_acc = running
            scores = jnp.einsum("qgnd,kgd->gqnk", q_grp, kv_blk[0], preferred_element_type=jnp.float32) * q_scale
            if keep_mask is not None:
                scores = jnp.where(keep_mask, scores, -jnp.inf)
            new_max = jnp.maximum(run_max, jnp.max(scores, axis=-1))
            p_blk = jnp.exp(scores - new_max[..., None])
            rescale = jnp.exp(run_max - new_max)
            new_sum = run_sum * rescale + jnp.sum(p_blk, axis=-1)
            new_acc = out_acc * rescale[..., None] + jnp.einsum("gqnk,kgd->gqnd", p_blk.astype(jnp.bfloat16), kv_blk[1], preferred_element_type=jnp.float32)
            return new_max, new_sum, new_acc

        stat_shape = (num_kv, tokens, group_size)
        initial = (jnp.full(stat_shape, -jnp.inf, jnp.float32), jnp.zeros(stat_shape, jnp.float32), jnp.zeros(stat_shape + (head_dim,), jnp.float32))
        kv_loc = jnp.stack([k_loc, v_loc])
        running = absorb(initial, kv_loc, diag_keep)

        def pass_step(hop_idx, loop_state):
            held_stats, kv_cur = loop_state
            kv_cur = lax.ppermute(kv_cur, CTX_AXES, next_rank)

            def visit(held):
                return absorb(held, kv_cur, None)

            def skip_block(held):
                return held

            held_stats = lax.cond(hop_idx <= my_rank, visit, skip_block, held_stats)
            return held_stats, kv_cur

        running, _ = lax.fori_loop(1, num_ranks, pass_step, (running, kv_loc))
        run_max, run_sum, out_acc = running
        out_blk = (out_acc / run_sum[..., None]).astype(jnp.bfloat16)
        return jnp.transpose(out_blk, (1, 0, 2, 3)).reshape(tokens, num_heads, head_dim)

    return jax.shard_map(local_attend, mesh=mesh, in_specs=(seq_spec, seq_spec, seq_spec), out_specs=seq_spec, check_vma=False)
```

profile of v0, /device:TPU:6, one launch (start us, length us, event | category | flops | bytes accessed | tf_op | source)
XLA Modules:
  0.0 98.4 jit_solution(10063052670222741108)
XLA Ops:
  0.0 1.7 %copy.13 = bf16[128,40,128]{2,0,1:T(8,128)(2,1)S(1)} copy(bf16[128,40,128]{2,1,0:T(8,128)(2,1)} %param.7) | data formatting | bytes 2621440 | tf_op args[0]
  5.3 90.3 %while.19 = (s32[]{:T(128)}, f32[8,128,5]{1,2,0:T(8,128)S(1)}, f32[8,128,5]{1,2,0:T(8,128)S(1)}, f32[8,128,5,128]{3,1,2,0:T(8,128)S(1)}, bf16[2,128,8,128]{3,1,2...) while((s32[]{:T(128)}, f32[8,128,5]{1,2,0:T(8,128)S(1)}, ...), condition=%wide.region_7.8_spmd, body=%wide.region_2.7_spmd.sunk | while | flops 342108160 | bytes 18440428 | solution.py:55
  5.3 8.6 %collective-permute-done = bf16[2,128,8,128]{3,1,2,0:T(8,128)(2,1)S(1)} collective-permute-done((bf16[2,128,8,128]{3,1,2,0:T(8,128)(2,1)}, bf16[2,128,8,128]{3,1,2,0:T(8,128)(2,1)S(1)}, u32[]{:S(2)}, u32[]{:S(2)}) %collective-permute-start) | collective-permute-done | bytes 524320 | tf_op jit(solution)/shard_map/while/body/eval_jaxpr/ppermute | solution.py:44
  13.9 4.1 %conditional.2 = ((f32[8,128,5]{1,2,0:T(8,128)S(1)}, f32[8,128,5]{1,2,0:T(8,128)S(1)}, f32[8,128,5,128]{3,1,2,0:T(8,128)S(1)})) conditional(s32[]{:T(128)} %convert_element_type.24, (f32[8,128,5]{1,2,0:T(8,128)S(1)}, f32[8,128,5]{1,2,0:T(8,128)S(1)}, f32[8,128,5,128]{3,1,2,0:T(8,128)S(1)}) %tuple.42, (bf16[2,128,8,128]{3,1,2,0:T(8,128)(2,1)S(1)}, ...), branch_computations={%region_3.3_spmd, %region_4.6_spmd} | conditional | flops 342108160 | bytes 15294496 | solution.py:52
  13.9 1.9 %multiply_reduce_fusion = (f32[8,128,5]{1,2,0:T(8,128)S(1)}, f32[8,128,5,128]{1,3,2,0:T(8,128)S(1)}) fusion(bf16[128,8,5,128]{3,0,2,1:T(8,128)(2,1)} %get-tuple-element.143, bf16[2,128,8,128]{3,1,2,0:T(8,128)(2,1)S(1)} %get-tuple-element.144), kind=kOutput, calls=%fused_computation.2 | convolution fusion | flops 169077760 | bytes 4214784 | tf_op jit(solution)/shard_map/while/body/eval_jaxpr/cond/branch_1_fun/qgnd,kgd->gqnk/dot_general | solution.py:27
  18.8 8.6 %collective-permute-done = bf16[2,128,8,128]{3,1,2,0:T(8,128)(2,1)S(1)} collective-permute-done((bf16[2,128,8,128]{3,1,2,0:T(8,128)(2,1)}, bf16[2,128,8,128]{3,1,2,0:T(8,128)(2,1)S(1)}, u32[]{:S(2)}, u32[]{:S(2)}) %collective-permute-start) | collective-permute-done | bytes 524320 | tf_op jit(solution)/shard_map/while/body/eval_jaxpr/ppermute | solution.py:44
  27.4 4.1 %conditional.2 = ((f32[8,128,5]{1,2,0:T(8,128)S(1)}, f32[8,128,5]{1,2,0:T(8,128)S(1)}, f32[8,128,5,128]{3,1,2,0:T(8,128)S(1)})) conditional(s32[]{:T(128)} %convert_element_type.24, (f32[8,128,5]{1,2,0:T(8,128)S(1)}, f32[8,128,5]{1,2,0:T(8,128)S(1)}, f32[8,128,5,128]{3,1,2,0:T(8,128)S(1)}) %tuple.42, (bf16[2,128,8,128]{3,1,2,0:T(8,128)(2,1)S(1)}, ...), branch_computations={%region_3.3_spmd, %region_4.6_spmd} | conditional | flops 342108160 | bytes 15294496 | solution.py:52
  27.4 1.9 %multiply_reduce_fusion = (f32[8,128,5]{1,2,0:T(8,128)S(1)}, f32[8,128,5,128]{1,3,2,0:T(8,128)S(1)}) fusion(bf16[128,8,5,128]{3,0,2,1:T(8,128)(2,1)} %get-tuple-element.143, bf16[2,128,8,128]{3,1,2,0:T(8,128)(2,1)S(1)} %get-tuple-element.144), kind=kOutput, calls=%fused_computation.2 | convolution fusion | flops 169077760 | bytes 4214784 | tf_op jit(solution)/shard_map/while/body/eval_jaxpr/cond/branch_1_fun/qgnd,kgd->gqnk/dot_general | solution.py:27
  32.3 8.6 %collective-permute-done = bf16[2,128,8,128]{3,1,2,0:T(8,128)(2,1)S(1)} collective-permute-done((bf16[2,128,8,128]{3,1,2,0:T(8,128)(2,1)}, bf16[2,128,8,128]{3,1,2,0:T(8,128)(2,1)S(1)}, u32[]{:S(2)}, u32[]{:S(2)}) %collective-permute-start) | collective-permute-done | bytes 524320 | tf_op jit(solution)/shard_map/while/body/eval_jaxpr/ppermute | solution.py:44
  40.9 4.1 %conditional.2 = ((f32[8,128,5]{1,2,0:T(8,128)S(1)}, f32[8,128,5]{1,2,0:T(8,128)S(1)}, f32[8,128,5,128]{3,1,2,0:T(8,128)S(1)})) conditional(s32[]{:T(128)} %convert_element_type.24, (f32[8,128,5]{1,2,0:T(8,128)S(1)}, f32[8,128,5]{1,2,0:T(8,128)S(1)}, f32[8,128,5,128]{3,1,2,0:T(8,128)S(1)}) %tuple.42, (bf16[2,128,8,128]{3,1,2,0:T(8,128)(2,1)S(1)}, ...), branch_computations={%region_3.3_spmd, %region_4.6_spmd} | conditional | flops 342108160 | bytes 15294496 | solution.py:52
  40.9 1.9 %multiply_reduce_fusion = (f32[8,128,5]{1,2,0:T(8,128)S(1)}, f32[8,128,5,128]{1,3,2,0:T(8,128)S(1)}) fusion(bf16[128,8,5,128]{3,0,2,1:T(8,128)(2,1)} %get-tuple-element.143, bf16[2,128,8,128]{3,1,2,0:T(8,128)(2,1)S(1)} %get-tuple-element.144), kind=kOutput, calls=%fused_computation.2 | convolution fusion | flops 169077760 | bytes 4214784 | tf_op jit(solution)/shard_map/while/body/eval_jaxpr/cond/branch_1_fun/qgnd,kgd->gqnk/dot_general | solution.py:27
  43.4 1.6 %multiply_add_fusion = f32[8,128,5,128]{3,1,2,0:T(8,128)S(1)} fusion(f32[8,128,5,128]{3,1,2,0:T(8,128)S(1)} %get-tuple-element.146, f32[8,128,5,128]{1,3,2,0:T(8,128)S(1)} %get-tuple-element.179, f32[8,128,5]{1,2,0:T(8,128)S(1)} %get-tuple-element.177, f32[8,128,5]{1,2,0:T(8,128)S(1)} %max.2, bf16[2,128,8,128]{3,1,2,0:T(8,128)(2,1)S(1)} %get-tuple-element.144), kind=kOutput, calls=%fused_computation | convolution fusion | flops 171048960 | bytes 8192000 | tf_op jit(solution)/shard_map/while/body/eval_jaxpr/cond/branch_1_fun/gqnk,kgd->gqnd/dot_general | solution.py:34
  45.8 8.6 %collective-permute-done = bf16[2,128,8,128]{3,1,2,0:T(8,128)(2,1)S(1)} collective-permute-done((bf16[2,128,8,128]{3,1,2,0:T(8,128)(2,1)}, bf16[2,128,8,128]{3,1,2,0:T(8,128)(2,1)S(1)}, u32[]{:S(2)}, u32[]{:S(2)}) %collective-permute-start) | collective-permute-done | bytes 524320 | tf_op jit(solution)/shard_map/while/body/eval_jaxpr/ppermute | solution.py:44
  54.4 4.1 %conditional.2 = ((f32[8,128,5]{1,2,0:T(8,128)S(1)}, f32[8,128,5]{1,2,0:T(8,128)S(1)}, f32[8,128,5,128]{3,1,2,0:T(8,128)S(1)})) conditional(s32[]{:T(128)} %convert_element_type.24, (f32[8,128,5]{1,2,0:T(8,128)S(1)}, f32[8,128,5]{1,2,0:T(8,128)S(1)}, f32[8,128,5,128]{3,1,2,0:T(8,128)S(1)}) %tuple.42, (bf16[2,128,8,128]{3,1,2,0:T(8,128)(2,1)S(1)}, ...), branch_computations={%region_3.3_spmd, %region_4.6_spmd} | conditional | flops 342108160 | bytes 15294496 | solution.py:52
  54.4 1.9 %multiply_reduce_fusion = (f32[8,128,5]{1,2,0:T(8,128)S(1)}, f32[8,128,5,128]{1,3,2,0:T(8,128)S(1)}) fusion(bf16[128,8,5,128]{3,0,2,1:T(8,128)(2,1)} %get-tuple-element.143, bf16[2,128,8,128]{3,1,2,0:T(8,128)(2,1)S(1)} %get-tuple-element.144), kind=kOutput, calls=%fused_computation.2 | convolution fusion | flops 169077760 | bytes 4214784 | tf_op jit(solution)/shard_map/while/body/eval_jaxpr/cond/branch_1_fun/qgnd,kgd->gqnk/dot_general | solution.py:27
  59.3 8.6 %collective-permute-done = bf16[2,128,8,128]{3,1,2,0:T(8,128)(2,1)S(1)} collective-permute-done((bf16[2,128,8,128]{3,1,2,0:T(8,128)(2,1)}, bf16[2,128,8,128]{3,1,2,0:T(8,128)(2,1)S(1)}, u32[]{:S(2)}, u32[]{:S(2)}) %collective-permute-start) | collective-permute-done | bytes 524320 | tf_op jit(solution)/shard_map/while/body/eval_jaxpr/ppermute | solution.py:44
  67.9 4.1 %conditional.2 = ((f32[8,128,5]{1,2,0:T(8,128)S(1)}, f32[8,128,5]{1,2,0:T(8,128)S(1)}, f32[8,128,5,128]{3,1,2,0:T(8,128)S(1)})) conditional(s32[]{:T(128)} %convert_element_type.24, (f32[8,128,5]{1,2,0:T(8,128)S(1)}, f32[8,128,5]{1,2,0:T(8,128)S(1)}, f32[8,128,5,128]{3,1,2,0:T(8,128)S(1)}) %tuple.42, (bf16[2,128,8,128]{3,1,2,0:T(8,128)(2,1)S(1)}, ...), branch_computations={%region_3.3_spmd, %region_4.6_spmd} | conditional | flops 342108160 | bytes 15294496 | solution.py:52
  67.9 1.9 %multiply_reduce_fusion = (f32[8,128,5]{1,2,0:T(8,128)S(1)}, f32[8,128,5,128]{1,3,2,0:T(8,128)S(1)}) fusion(bf16[128,8,5,128]{3,0,2,1:T(8,128)(2,1)} %get-tuple-element.143, bf16[2,128,8,128]{3,1,2,0:T(8,128)(2,1)S(1)} %get-tuple-element.144), kind=kOutput, calls=%fused_computation.2 | convolution fusion | flops 169077760 | bytes 4214784 | tf_op jit(solution)/shard_map/while/body/eval_jaxpr/cond/branch_1_fun/qgnd,kgd->gqnk/dot_general | solution.py:27
  72.8 8.6 %collective-permute-done = bf16[2,128,8,128]{3,1,2,0:T(8,128)(2,1)S(1)} collective-permute-done((bf16[2,128,8,128]{3,1,2,0:T(8,128)(2,1)}, bf16[2,128,8,128]{3,1,2,0:T(8,128)(2,1)S(1)}, u32[]{:S(2)}, u32[]{:S(2)}) %collective-permute-start) | collective-permute-done | bytes 524320 | tf_op jit(solution)/shard_map/while/body/eval_jaxpr/ppermute | solution.py:44
  81.4 4.1 %conditional.2 = ((f32[8,128,5]{1,2,0:T(8,128)S(1)}, f32[8,128,5]{1,2,0:T(8,128)S(1)}, f32[8,128,5,128]{3,1,2,0:T(8,128)S(1)})) conditional(s32[]{:T(128)} %convert_element_type.24, (f32[8,128,5]{1,2,0:T(8,128)S(1)}, f32[8,128,5]{1,2,0:T(8,128)S(1)}, f32[8,128,5,128]{3,1,2,0:T(8,128)S(1)}) %tuple.42, (bf16[2,128,8,128]{3,1,2,0:T(8,128)(2,1)S(1)}, ...), branch_computations={%region_3.3_spmd, %region_4.6_spmd} | conditional | flops 342108160 | bytes 15294496 | solution.py:52
  81.4 1.9 %multiply_reduce_fusion = (f32[8,128,5]{1,2,0:T(8,128)S(1)}, f32[8,128,5,128]{1,3,2,0:T(8,128)S(1)}) fusion(bf16[128,8,5,128]{3,0,2,1:T(8,128)(2,1)} %get-tuple-element.143, bf16[2,128,8,128]{3,1,2,0:T(8,128)(2,1)S(1)} %get-tuple-element.144), kind=kOutput, calls=%fused_computation.2 | convolution fusion | flops 169077760 | bytes 4214784 | tf_op jit(solution)/shard_map/while/body/eval_jaxpr/cond/branch_1_fun/qgnd,kgd->gqnk/dot_general | solution.py:27
  83.9 1.6 %multiply_add_fusion = f32[8,128,5,128]{3,1,2,0:T(8,128)S(1)} fusion(f32[8,128,5,128]{3,1,2,0:T(8,128)S(1)} %get-tuple-element.146, f32[8,128,5,128]{1,3,2,0:T(8,128)S(1)} %get-tuple-element.179, f32[8,128,5]{1,2,0:T(8,128)S(1)} %get-tuple-element.177, f32[8,128,5]{1,2,0:T(8,128)S(1)} %max.2, bf16[2,128,8,128]{3,1,2,0:T(8,128)(2,1)S(1)} %get-tuple-element.144), kind=kOutput, calls=%fused_computation | convolution fusion | flops 171048960 | bytes 8192000 | tf_op jit(solution)/shard_map/while/body/eval_jaxpr/cond/branch_1_fun/gqnk,kgd->gqnd/dot_general | solution.py:34
  86.2 8.6 %collective-permute-done = bf16[2,128,8,128]{3,1,2,0:T(8,128)(2,1)S(1)} collective-permute-done((bf16[2,128,8,128]{3,1,2,0:T(8,128)(2,1)}, bf16[2,128,8,128]{3,1,2,0:T(8,128)(2,1)S(1)}, u32[]{:S(2)}, u32[]{:S(2)}) %collective-permute-start) | collective-permute-done | bytes 524320 | tf_op jit(solution)/shard_map/while/body/eval_jaxpr/ppermute | solution.py:44
  96.5 1.9 %copy.19 = bf16[128,40,128]{2,1,0:T(8,128)(2,1)} copy(bf16[128,40,128]{2,0,1:T(8,128)(2,1)S(1)} %bitcast.28) | data formatting | bytes 2621440 | tf_op jit(solution)/shard_map/reshape | solution.py:58
  (57 shorter events, 19.4 us)
Async XLA Ops:
  0.0 1.7 %copy-start.1 = (bf16[128,8,128]{2,1,0:T(8,128)(2,1)S(1)}, bf16[128,8,128]{2,1,0:T(8,128)(2,1)}, u32[]{:S(2)}) copy-start(bf16[128,8,128]{2,1,0:T(8,128)(2,1)} %param.8) | copy-start | bytes 786436
  1.7 1.3 %copy-start = (bf16[128,40,128]{2,0,1:T(8,128)(2,1)}, bf16[128,40,128]{2,0,1:T(8,128)(2,1)S(1)}, u32[]{:S(2)}) copy-start(bf16[128,40,128]{2,0,1:T(8,128)(2,1)S(1)} %copy.13) | copy-start | bytes 3932164
  1.7 1.3 %copy-start.2 = (bf16[128,8,128]{2,1,0:T(8,128)(2,1)S(1)}, bf16[128,8,128]{2,1,0:T(8,128)(2,1)}, u32[]{:S(2)}) copy-start(bf16[128,8,128]{2,1,0:T(8,128)(2,1)} %param.9) | copy-start | bytes 786436
  5.3 8.6 %collective-permute-start = (bf16[2,128,8,128]{3,1,2,0:T(8,128)(2,1)}, bf16[2,128,8,128]{3,1,2,0:T(8,128)(2,1)S(1)}, u32[]{:S(2)}, u32[]{:S(2)}) collective-permute-start(bf16[2,128,8,128]{3,1,2,0:T(8,128)(2,1)} %get-tuple-element.253), channel_id=1, source_target_pairs={{0,1},{1,2},{2,3},{3,4},{4,5},{5,6},{6,7},{7,0}} | collective-permute-start | bytes 1572872 | tf_op jit(solution)/shard_map/while/body/eval_jaxpr/ppermute | solution.py:44
  18.8 8.6 %collective-permute-start = (bf16[2,128,8,128]{3,1,2,0:T(8,128)(2,1)}, bf16[2,128,8,128]{3,1,2,0:T(8,128)(2,1)S(1)}, u32[]{:S(2)}, u32[]{:S(2)}) collective-permute-start(bf16[2,128,8,128]{3,1,2,0:T(8,128)(2,1)} %get-tuple-element.253), channel_id=1, source_target_pairs={{0,1},{1,2},{2,3},{3,4},{4,5},{5,6},{6,7},{7,0}} | collective-permute-start | bytes 1572872 | tf_op jit(solution)/shard_map/while/body/eval_jaxpr/ppermute | solution.py:44
  32.3 8.6 %collective-permute-start = (bf16[2,128,8,128]{3,1,2,0:T(8,128)(2,1)}, bf16[2,128,8,128]{3,1,2,0:T(8,128)(2,1)S(1)}, u32[]{:S(2)}, u32[]{:S(2)}) collective-permute-start(bf16[2,128,8,128]{3,1,2,0:T(8,128)(2,1)} %get-tuple-element.253), channel_id=1, source_target_pairs={{0,1},{1,2},{2,3},{3,4},{4,5},{5,6},{6,7},{7,0}} | collective-permute-start | bytes 1572872 | tf_op jit(solution)/shard_map/while/body/eval_jaxpr/ppermute | solution.py:44
  45.8 8.6 %collective-permute-start = (bf16[2,128,8,128]{3,1,2,0:T(8,128)(2,1)}, bf16[2,128,8,128]{3,1,2,0:T(8,128)(2,1)S(1)}, u32[]{:S(2)}, u32[]{:S(2)}) collective-permute-start(bf16[2,128,8,128]{3,1,2,0:T(8,128)(2,1)} %get-tuple-element.253), channel_id=1, source_target_pairs={{0,1},{1,2},{2,3},{3,4},{4,5},{5,6},{6,7},{7,0}} | collective-permute-start | bytes 1572872 | tf_op jit(solution)/shard_map/while/body/eval_jaxpr/ppermute | solution.py:44
  59.3 8.6 %collective-permute-start = (bf16[2,128,8,128]{3,1,2,0:T(8,128)(2,1)}, bf16[2,128,8,128]{3,1,2,0:T(8,128)(2,1)S(1)}, u32[]{:S(2)}, u32[]{:S(2)}) collective-permute-start(bf16[2,128,8,128]{3,1,2,0:T(8,128)(2,1)} %get-tuple-element.253), channel_id=1, source_target_pairs={{0,1},{1,2},{2,3},{3,4},{4,5},{5,6},{6,7},{7,0}} | collective-permute-start | bytes 1572872 | tf_op jit(solution)/shard_map/while/body/eval_jaxpr/ppermute | solution.py:44
  72.8 8.6 %collective-permute-start = (bf16[2,128,8,128]{3,1,2,0:T(8,128)(2,1)}, bf16[2,128,8,128]{3,1,2,0:T(8,128)(2,1)S(1)}, u32[]{:S(2)}, u32[]{:S(2)}) collective-permute-start(bf16[2,128,8,128]{3,1,2,0:T(8,128)(2,1)} %get-tuple-element.253), channel_id=1, source_target_pairs={{0,1},{1,2},{2,3},{3,4},{4,5},{5,6},{6,7},{7,0}} | collective-permute-start | bytes 1572872 | tf_op jit(solution)/shard_map/while/body/eval_jaxpr/ppermute | solution.py:44
  86.2 8.6 %collective-permute-start = (bf16[2,128,8,128]{3,1,2,0:T(8,128)(2,1)}, bf16[2,128,8,128]{3,1,2,0:T(8,128)(2,1)S(1)}, u32[]{:S(2)}, u32[]{:S(2)}) collective-permute-start(bf16[2,128,8,128]{3,1,2,0:T(8,128)(2,1)} %get-tuple-element.253), channel_id=1, source_target_pairs={{0,1},{1,2},{2,3},{3,4},{4,5},{5,6},{6,7},{7,0}} | collective-permute-start | bytes 1572872 | tf_op jit(solution)/shard_map/while/body/eval_jaxpr/ppermute | solution.py:44
where the time goes:
time: 98.7 us; the launch traced here: 98.4 us
  waiting for transfers between devices  60.2 us (61%)
  matrix products  23 us (23%)
  local copies, waits for them, and re-layouts  9.16 us (9%)
  other arithmetic  5.59 us (6%)
    ppermute x7, waiting for transfers between devices, pass_step(): kv_cur = lax.ppermute(kv_cur, CTX_AXES, next_rank)  60.2 us
    dot_general x7, matrix products, absorb(): jnp.einsum('qgnd,kgd->gqnk', q_grp, kv_blk[0], preferred_element_type=jnp...  12.2 us
    dot_general x7, matrix products, absorb(): jnp.einsum('gqnk,kgd->gqnd', p_blk.astype(jnp.bfloat16), kv_blk[1], prefe...  10.8 us
    while x7, local copies, waits for them, and re-layouts  5.46 us
    reduce_sum x7, other arithmetic, absorb(): new_sum = run_sum * rescale + jnp.sum(p_blk, axis=-1)  3.72 us
  transfers between devices with their start and end apart: 7, of which 7 were waited for; matrix products, arithmetic and copies ran while one was open for 0% of the time, Pallas kernels for 0%

commit v1 on v0

v1 whole, which is shorter than its diff:
```python
import functools
import math

import jax
import jax.numpy as jnp
from jax import lax
from jax.experimental import pallas as pl
from jax.experimental.pallas import tpu as pltpu
from jax.sharding import PartitionSpec as P

MESH = pl.DeviceIdType.MESH
F32 = jnp.float32
BF16 = jnp.bfloat16

K_UNITS = ((0, 4, 0), (4, 4, 1))
V_UNITS = tuple((h, 1, h % 2) for h in range(8))
NK, NV = len(K_UNITS), len(V_UNITS)
NU = NK + NV
X, Y, Z, PT, PX, PY, PZ = range(7)
OWN = 3


def kernel(q_hbm, k_hbm, v_hbm, o_ref, kbuf, vbuf, qt, s_buf, p_buf, mp, linv, q_raw, k_raw, v_raw, f_buf, o32, lsem, ssem, rsem):
    tokens, num_heads, dim = q_hbm.shape
    num_kv = k_hbm.shape[1]
    group = num_heads // num_kv
    rows = group * tokens
    pair = 2 * tokens
    iy, cy = lax.axis_index("cx"), lax.axis_index("cy")
    ix, core = cy // 2, cy % 2
    cy_x = (cy + 2) % 4
    cy_p = cy + 1 - 2 * core
    cy_xp = (cy_p + 2) % 4
    iy_o = 1 - iy
    rank_of = {OWN + 10: iy * 4 + cy, X: iy * 4 + cy_x, Y: iy_o * 4 + cy, Z: iy_o * 4 + cy_x, PT: iy * 4 + cy_p, PX: iy * 4 + cy_xp, PY: iy_o * 4 + cy_p, PZ: iy_o * 4 + cy_xp}
    ME = OWN + 10
    dev_x, dev_y, dev_p = (0, iy, cy_x), (0, iy_o, cy), (0, iy, cy_p)
    chip_of = {X: iy * 2 + 1 - ix, Y: iy_o * 2 + ix, Z: iy_o * 2 + 1 - ix, OWN: iy * 2 + ix}

    loads = [pltpu.make_async_copy(k_hbm, k_raw, lsem.at[0]), pltpu.make_async_copy(v_hbm, v_raw, lsem.at[1]), pltpu.make_async_copy(q_hbm, q_raw, lsem.at[2])]
    for load in loads:
        load.start()
    barrier = pltpu.get_barrier_semaphore()
    for dev in (dev_x, dev_y, dev_p):
        pl.semaphore_signal(barrier, inc=1, device_id=dev, device_id_type=MESH)

    def split_heads(raw, heads, put):
        step = 32

        def widen(i, carry):
            t = pl.multiple_of(i * step, step)
            f_buf[pl.ds(pl.multiple_of(t * heads, step * heads), step * heads), :] = raw[pl.ds(t, step)].astype(F32).reshape(step * heads, dim)
            return carry

        lax.fori_loop(0, tokens // step, widen, 0)
        for h in range(heads):
            put(h, f_buf[pl.ds(h, tokens, stride=heads), :].astype(BF16))

    my_rows = pl.ds(pl.multiple_of(rank_of[ME] * tokens, tokens), tokens)

    def put_k(h, val):
        kbuf[h, my_rows, :] = val

    def put_v(h, val):
        vbuf[h, my_rows, :] = val

    def put_q(h, val):
        qt[h // group, pl.ds((h % group) * tokens, tokens), :] = val

    loads[0].wait()
    split_heads(k_raw, num_kv, put_k)
    loads[1].wait()
    split_heads(v_raw, num_kv, put_v)
    pl.semaphore_wait(barrier, 3)

    sends = []

    def piece(unit, src):
        buf, (h0, n, _) = (kbuf, K_UNITS[unit]) if unit < NK else (vbuf, V_UNITS[unit - NK])
        return buf.at[pl.ds(h0, n), pl.ds(pl.multiple_of(rank_of[src] * tokens, tokens), tokens), :]

    def send(unit, src, dev, as_src):
        ref = piece(unit, src)
        copy = pltpu.make_async_remote_copy(ref, ref, ssem.at[len(sends)], rsem.at[as_src * NU + unit], device_id=dev, device_id_type=MESH)
        copy.start()
        sends.append(copy)

    def arrive(unit, src):
        ref = piece(unit, src)
        pltpu.make_async_remote_copy(ref, ref, ssem.at[0], rsem.at[src * NU + unit], device_id=dev_p, device_id_type=MESH).wait_recv()

    def path(unit):
        return (K_UNITS + V_UNITS)[unit][2]

    def own_link(unit, which):
        send(unit, ME, (dev_x, dev_y)[which], (X, Y)[which])

    def take(unit, src, relay=True):
        arrive(unit, src)
        if src == X and path(unit) == 0 and relay:
            send(unit, X, dev_y, Z)
        if src == Y and path(unit) == 1 and relay:
            send(unit, Y, dev_x, Z)
        send(unit, src, dev_p, {X: PX, Y: PY, Z: PZ}[src])

    own_link(0, 0)
    own_link(1, 1)
    own_link(1, 0)
    own_link(0, 1)
    for u in range(NU):
        send(u, ME, dev_p, PT)

    loads[2].wait()
    split_heads(q_raw, num_heads, put_q)

    def scores(blk, h):
        kk = kbuf[h, pl.ds(pl.multiple_of(chip_of[blk] * pair, pair), pair), :]
        return lax.dot_general(qt[h], kk, (((1,), (1,)), ((), ())), preferred_element_type=F32)

    def score_own(h):
        s = scores(OWN, h)
        q_pos = lax.broadcasted_iota(jnp.int32, (rows, pair), 0) % tokens + core * tokens
        k_pos = lax.broadcasted_iota(jnp.int32, (rows, pair), 1)
        s = jnp.where(k_pos <= q_pos, s, -jnp.inf)
        s_buf[OWN, h] = s
        mp[h] = jnp.maximum(s[:, :tokens], s[:, tokens:])

    def score_other(blk, h):
        s = scores(blk, h)
        s_buf[blk, h] = s
        mp[h] = jnp.maximum(mp[h], jnp.maximum(s[:, :tokens], s[:, tokens:]))

    def for_heads(h0, n, body):
        def step(h, carry):
            body(h)
            return carry

        lax.fori_loop(h0, h0 + n, step, 0)

    needed = {X: ix == 1, Y: iy == 1, Z: iy == 1}

    def scores_of(blk, unit):
        h0, n, _ = K_UNITS[unit]
        arrive(unit, {X: PX, Y: PY, Z: PZ}[blk])

        @pl.when(needed[blk])
        def _():
            for_heads(h0, n, functools.partial(score_other, blk))

    for u in range(NK):
        arrive(u, PT)
    for_heads(0, num_kv, score_own)

    take(0, X)
    take(1, Y)
    for v in (0, 1):
        own_link(NK + v, 0)
        own_link(NK + v, 1)
    scores_of(X, 0)
    scores_of(Y, 1)
    take(1, X)
    take(0, Y)
    scores_of(X, 1)
    scores_of(Y, 0)
    take(0, Z)
    take(1, Z)
    scores_of(Z, 0)
    scores_of(Z, 1)

    log2_scale = dim ** -0.5 * math.log2(math.e)
    step_rows = 64

    def probs(h):
        def chunk(i, carry):
            r = pl.ds(pl.multiple_of(i * step_rows, step_rows), step_rows)
            m = jnp.max(mp[h, r, :], axis=-1, keepdims=True) * log2_scale
            total = jnp.zeros((step_rows, tokens), F32)

            def one(blk, total):
                p = jnp.exp2(s_buf[blk, h, r, :] * log2_scale - m)
                p_buf[blk, h, r, :] = p.astype(BF16)
                return total + (p[:, :tokens] + p[:, tokens:])

            total = one(OWN, total)
            for blk in (X, Y, Z):
                def none(blk, total):
                    p_buf[blk, h, r, :] = jnp.zeros((step_rows, pair), BF16)
                    return total

                total = lax.cond(needed[blk], functools.partial(one, blk), functools.partial(none, blk), total)
            linv[h, r, :] = 1.0 / jnp.broadcast_to(jnp.sum(total, axis=-1, keepdims=True), (step_rows, dim))
            return carry

        lax.fori_loop(0, rows // step_rows, chunk, 0)

    def outputs(h):
        acc = None
        for blk in (OWN, X, Y, Z):
            vv = vbuf[h, pl.ds(pl.multiple_of(chip_of[blk] * pair, pair), pair), :]
            part = lax.dot_general(p_buf[blk, h], vv, (((1,), (0,)), ((), ())), preferred_element_type=F32)
            acc = part if acc is None else acc + part
        out = acc * linv[h]
        for n in range(group):
            o32[pl.ds(h * group + n, tokens, stride=num_heads), :] = out[n * tokens : (n + 1) * tokens, :]

    def finish(v):
        for src in (PT, PX, PY, PZ):
            arrive(NK + v, src)
        h0, n, _ = V_UNITS[v]
        for h in range(h0, h0 + n):
            outputs(h)

    for v in range(NV):
        take(NK + v, X)
        take(NK + v, Y)
        if v + 2 < NV:
            own_link(NK + v + 2, 0)
            own_link(NK + v + 2, 1)
        if v >= 2:
            take(NK + v - 2, Z)
        h0, n, _ = V_UNITS[v]
        for_heads(h0, n, probs)
        if v >= 3:
            finish(v - 3)
    take(NK + NV - 2, Z)
    finish(NV - 3)
    take(NK + NV - 1, Z)
    finish(NV - 2)
    finish(NV - 1)

    def narrow(i, carry):
        t = pl.multiple_of(i * 16, 16)
        o_ref[pl.ds(t, 16)] = o32[pl.ds(pl.multiple_of(t * num_heads, 16 * num_heads), 16 * num_heads), :].reshape(16, num_heads, dim).astype(BF16)
        return carry

    lax.fori_loop(0, tokens // 16, narrow, 0)
    for copy in sends:
        copy.wait_send()


def solution(mesh):
    seq_spec = P(("batch", "cx", "cy"), None, None)
    ranks = mesh.shape["cx"] * mesh.shape["cy"]

    def local(q, k, v):
        tokens, heads, dim = q.shape
        kv = k.shape[1]
        rows = heads // kv * tokens
        n_sends = 3 * NU + NU + 3 * NU
        hbm = pl.BlockSpec(memory_space=pltpu.HBM)
        return pl.pallas_call(
            kernel,
            out_shape=jax.ShapeDtypeStruct(q.shape, q.dtype),
            in_specs=[hbm, hbm, hbm],
            out_specs=pl.BlockSpec(memory_space=pltpu.VMEM),
            scratch_shapes=[
                pltpu.VMEM((kv, ranks * tokens, dim), BF16),
                pltpu.VMEM((kv, ranks * tokens, dim), BF16),
                pltpu.VMEM((kv, rows, dim), BF16),
                pltpu.VMEM((4, kv, rows, 2 * tokens), F32),
                pltpu.VMEM((4, kv, rows, 2 * tokens), BF16),
                pltpu.VMEM((kv, rows, dim), F32),
                pltpu.VMEM((kv, rows, dim), F32),
                pltpu.VMEM((tokens, heads, dim), BF16),
                pltpu.VMEM((tokens, kv, dim), BF16),
                pltpu.VMEM((tokens, kv, dim), BF16),
                pltpu.VMEM((tokens * heads, dim), F32),
                pltpu.VMEM((tokens * heads, dim), F32),
                pltpu.SemaphoreType.DMA((3,)),
                pltpu.SemaphoreType.DMA((n_sends,)),
                pltpu.SemaphoreType.DMA((7 * NU,)),
            ],
            compiler_params=pltpu.CompilerParams(collective_id=0, has_side_effects=True, vmem_limit_bytes=56 * 2**20),
        )(q, k, v)

    return jax.shard_map(local, mesh=mesh, in_specs=(seq_spec, seq_spec, seq_spec), out_specs=seq_spec, check_vma=False)
```

time: 98.7 us -> 45.7 us (0.46)
  the two profiles are of different devices: /device:TPU:6 before, /device:TPU:7 now
where the time goes in v1:
time: 45.7 us; the launch traced here: 45.6 us
  Pallas kernels  43.1 us (94%)
  local copies, waits for them, and re-layouts  2.49 us (5%)
    pallas_call x1, Pallas kernels, local(): pl.pallas_call(kernel, out_shape=jax.ShapeDtypeStruct(q.shape, q.dtype),...  43.1 us
    unnamed x1, local copies, waits for them, and re-layouts  2.49 us

profile of v1, /device:TPU:7, one launch (start us, length us, event | category | flops | bytes accessed | tf_op | source)
XLA Modules:
  0.0 45.6 jit_solution(4962909475759839696)
XLA Ops:
  0.0 43.1 %shard_map.37 = bf16[128,40,128]{2,1,0:T(8,128)(2,1)} custom-call(bf16[128,40,128]{2,1,0:T(8,128)(2,1)} %q_hbm.1, bf16[128,8,128]{2,1,0:T(8,128)(2,1)} %k_hbm.1, bf16[128,8,128]{2,1,0:T(8,128)(2,1)} %v_hbm.1), custom_call_target="tpu_custom_call" | custom-call | tf_op jit(solution)/shard_map/pallas_call | solution.py:251
  43.1 2.5 %copy.5 = bf16[128,40,128]{2,1,0:T(8,128)(2,1)} copy(bf16[128,40,128]{2,1,0:T(8,128)(2,1)} %shard_map.37) | data formatting | bytes 2621440

commit v2 on v1

v2 whole, which is shorter than its diff:
```python
import math

import jax
import jax.numpy as jnp
from jax import lax
from jax.experimental import pallas as pl
from jax.experimental.pallas import tpu as pltpu
from jax.sharding import PartitionSpec as P

MESH = pl.DeviceIdType.MESH
F32 = jnp.float32
BF16 = jnp.bfloat16

K_UNITS = ((0, 4, 0), (4, 4, 1))
V_UNITS = ((0, 2, 0), (2, 2, 1), (4, 2, 0), (6, 2, 1))
W_UNITS = tuple((h, 1, (h // 2) % 2) for h in range(8))
NK, NV, NW = len(K_UNITS), len(V_UNITS), len(W_UNITS)
UNITS = K_UNITS + V_UNITS + W_UNITS
NU = len(UNITS)
X, Y, Z, OWN = range(4)
PT, PX, PY, PZ = 3, 4, 5, 6
ME = 7
ROLE_BLOCKS = ((OWN,), (OWN, X), (OWN, Y, Z), (OWN, X, Y, Z))


def kernel(q_hbm, k_hbm, v_hbm, o_ref, kbuf, vbuf, qt, s_buf, p_buf, mp, lsum, acc, q_raw, k_raw, v_raw, f_buf, lsem, ssem, rsem):
    tokens, num_heads, dim = q_hbm.shape
    num_kv = k_hbm.shape[1]
    group = num_heads // num_kv
    rows = group * tokens
    pair = 2 * tokens
    iy, cy = lax.axis_index("cx"), lax.axis_index("cy")
    ix, core = cy // 2, cy % 2
    chip = iy * 2 + ix
    cy_x = (cy + 2) % 4
    cy_p = cy + 1 - 2 * core
    cy_xp = (cy_p + 2) % 4
    iy_o = 1 - iy
    rank_of = {ME: iy * 4 + cy, X: iy * 4 + cy_x, Y: iy_o * 4 + cy, Z: iy_o * 4 + cy_x, PT: iy * 4 + cy_p, PX: iy * 4 + cy_xp, PY: iy_o * 4 + cy_p, PZ: iy_o * 4 + cy_xp}
    dev_x, dev_y, dev_p = (0, iy, cy_x), (0, iy_o, cy), (0, iy, cy_p)
    chip_of = {X: iy * 2 + 1 - ix, Y: iy_o * 2 + ix, Z: iy_o * 2 + 1 - ix, OWN: chip}

    loads = [pltpu.make_async_copy(k_hbm, k_raw, lsem.at[0]), pltpu.make_async_copy(v_hbm, v_raw, lsem.at[1]), pltpu.make_async_copy(q_hbm, q_raw, lsem.at[2])]
    for load in loads:
        load.start()
    barrier = pltpu.get_barrier_semaphore()
    for dev in (dev_x, dev_y, dev_p):
        pl.semaphore_signal(barrier, inc=1, device_id=dev, device_id_type=MESH)

    def split_heads(raw, heads, put):
        step = 32

        def widen(i, carry):
            t = pl.multiple_of(i * step, step)
            f_buf[pl.ds(pl.multiple_of(t * heads, step * heads), step * heads), :] = raw[pl.ds(t, step)].astype(F32).reshape(step * heads, dim)
            return carry

        lax.fori_loop(0, tokens // step, widen, 0)
        for h in range(heads):
            put(h, f_buf[pl.ds(h, tokens, stride=heads), :].astype(BF16))

    my_rows = pl.ds(pl.multiple_of(rank_of[ME] * tokens, tokens), tokens)

    def put_k(h, val):
        kbuf[h, my_rows, :] = val

    def put_v(h, val):
        vbuf[h, my_rows, :] = val

    def put_q(h, val):
        qt[h // group, pl.ds((h % group) * tokens, tokens), :] = val

    sends = []

    def piece(unit, src):
        h0, n, _ = UNITS[unit]
        buf = kbuf if unit < NK else vbuf
        return buf.at[pl.ds(h0, n), pl.ds(pl.multiple_of(rank_of[src] * tokens, tokens), tokens), :]

    def send(unit, src, dev, as_src):
        ref = piece(unit, src)
        copy = pltpu.make_async_remote_copy(ref, ref, ssem.at[len(sends)], rsem.at[as_src * NU + unit], device_id=dev, device_id_type=MESH)
        copy.start()
        sends.append(copy)

    def arrive(unit, src):
        ref = piece(unit, src)
        pltpu.make_async_remote_copy(ref, ref, ssem.at[0], rsem.at[src * NU + unit], device_id=dev_p, device_id_type=MESH).wait_recv()

    def own_link(unit, which):
        send(unit, ME, (dev_x, dev_y)[which], (X, Y)[which])

    def share(unit, src):
        send(unit, src, dev_p, {X: PX, Y: PY, Z: PZ}[src])

    def relay(unit, src):
        send(unit, src, {X: dev_y, Y: dev_x}[src], Z)

    def by_role(body):
        for role, blocks in enumerate(ROLE_BLOCKS):
            @pl.when(chip == role)
            def _():
                body(blocks)

    def scores(blk, h):
        kk = kbuf[h, pl.ds(pl.multiple_of(chip_of[blk] * pair, pair), pair), :]
        return lax.dot_general(qt[h], kk, (((1,), (1,)), ((), ())), preferred_element_type=F32)

    def score_own(h):
        s = scores(OWN, h)
        q_pos = lax.broadcasted_iota(jnp.int32, (rows, pair), 0) % tokens + core * tokens
        k_pos = lax.broadcasted_iota(jnp.int32, (rows, pair), 1)
        s = jnp.where(k_pos <= q_pos, s, -jnp.inf)
        s_buf[OWN, h] = s
        mp[h] = jnp.maximum(s[:, :tokens], s[:, tokens:])

    def score_other(blk, h):
        s = scores(blk, h)
        s_buf[blk, h] = s
        mp[h] = jnp.maximum(mp[h], jnp.maximum(s[:, :tokens], s[:, tokens:]))

    needed = {X: ix == 1, Y: iy == 1, Z: iy == 1}

    def scores_of(blk, unit):
        h0, n, _ = K_UNITS[unit]

        @pl.when(needed[blk])
        def _():
            for h in range(h0, h0 + n):
                score_other(blk, h)

    loads[0].wait()
    split_heads(k_raw, num_kv, put_k)
    pl.semaphore_wait(barrier, 3)
    own_link(0, 0)
    own_link(1, 1)
    own_link(1, 0)
    own_link(0, 1)
    for u in range(NK):
        send(u, ME, dev_p, PT)
    loads[1].wait()
    split_heads(v_raw, num_kv, put_v)
    loads[2].wait()
    split_heads(q_raw, num_heads, put_q)
    for u in range(NK):
        arrive(u, PT)
    for h in range(num_kv):
        score_own(h)

    arrive(0, X)
    relay(0, X)
    arrive(1, Y)
    relay(1, Y)
    share(0, X)
    share(1, Y)
    for a, b in ((0, 1), (1, 0), (2, 3), (3, 2)):
        own_link(NK + a, 0)
        own_link(NK + b, 1)
    for u in range(NV):
        send(NK + u, ME, dev_p, PT)
    arrive(0, PX)
    scores_of(X, 0)
    arrive(1, PY)
    scores_of(Y, 1)
    arrive(1, X)
    share(1, X)
    arrive(0, Y)
    share(0, Y)
    arrive(1, PX)
    scores_of(X, 1)
    arrive(0, PY)
    scores_of(Y, 0)
    arrive(0, Z)
    share(0, Z)
    arrive(1, Z)
    share(1, Z)
    arrive(0, PZ)
    scores_of(Z, 0)
    arrive(1, PZ)
    scores_of(Z, 1)

    log2_scale = dim ** -0.5 * math.log2(math.e)
    step_rows = 64

    def row_max(h):
        mp[h] = jnp.broadcast_to(jnp.max(mp[h], axis=-1, keepdims=True) * log2_scale, (rows, tokens))

    def probs(h, blocks):
        for r0 in range(0, rows, step_rows):
            r = pl.ds(r0, step_rows)
            m = mp[h, r, :]
            total = None
            for blk in blocks:
                for c0 in (0, tokens):
                    p = jnp.exp2(s_buf[blk, h, r, pl.ds(c0, tokens)] * log2_scale - m)
                    p_buf[blk, h, r, pl.ds(c0, tokens)] = p.astype(BF16)
                    total = p if total is None else total + p
            lsum[h, r, :] = total

    def row_sum(h):
        lsum[h] = jnp.broadcast_to(1.0 / jnp.sum(lsum[h], axis=-1, keepdims=True), (rows, dim))

    def weighted(h, blocks):
        total = None
        for blk in blocks:
            vv = vbuf[h, pl.ds(pl.multiple_of(chip_of[blk] * pair, pair), pair), :]
            part = lax.dot_general(p_buf[blk, h], vv, (((1,), (0,)), ((), ())), preferred_element_type=F32)
            total = part if total is None else total + part
        return total

    def near(h, blocks):
        acc[h] = weighted(h, [blk for blk in blocks if blk != Z])

    def last(h, blocks):
        out = acc[h] if Z not in blocks else acc[h] + weighted(h, [Z])
        out = out * lsum[h]
        for n in range(group):
            f_buf[pl.ds(h * group + n, tokens, stride=num_heads), :] = out[n * tokens : (n + 1) * tokens, :]

    def values_from_links(u):
        arrive(NK + u, X)
        arrive(NK + u, Y)
        h0, n, path = V_UNITS[u]
        for h in range(h0, h0 + n):
            relay(NK + NV + h, (X, Y)[path])
        share(NK + u, X)
        share(NK + u, Y)

    def values_from_partner(u):
        for src in (PT, PX, PY):
            arrive(NK + u, src)

    def stage(h):
        def body(blocks):
            if h == 0:
                row_max(0)
            if h + 1 < num_kv:
                row_max(h + 1)
            if h < num_kv:
                probs(h, blocks)
            if h > 0:
                row_sum(h - 1)

        by_role(body)

    def near_stage(u):
        h0, n, _ = V_UNITS[u]

        def body(blocks):
            for h in range(h0, h0 + n):
                near(h, blocks)

        by_role(body)

    for u in range(NV):
        stage(2 * u)
        values_from_links(u)
        stage(2 * u + 1)
        if u > 0:
            values_from_partner(u - 1)
            near_stage(u - 1)
    stage(num_kv)
    values_from_partner(NV - 1)
    near_stage(NV - 1)
    order = (0, 2, 1, 3, 4, 6, 5, 7)
    for i, h in enumerate(order):
        arrive(NK + NV + h, Z)
        share(NK + NV + h, Z)
        if i > 0:
            g = order[i - 1]
            arrive(NK + NV + g, PZ)
            by_role(lambda blocks: last(g, blocks))
    arrive(NK + NV + order[-1], PZ)
    by_role(lambda blocks: last(order[-1], blocks))

    def narrow(i, carry):
        t = pl.multiple_of(i * 16, 16)
        o_ref[pl.ds(t, 16)] = f_buf[pl.ds(pl.multiple_of(t * num_heads, 16 * num_heads), 16 * num_heads), :].reshape(16, num_heads, dim).astype(BF16)
        return carry

    lax.fori_loop(0, tokens // 16, narrow, 0)
    for copy in sends:
        copy.wait_send()


def solution(mesh):
    seq_spec = P(("batch", "cx", "cy"), None, None)
    ranks = mesh.shape["cx"] * mesh.shape["cy"]

    def local(q, k, v):
        tokens, heads, dim = q.shape
        kv = k.shape[1]
        rows = heads // kv * tokens
        hbm = pl.BlockSpec(memory_space=pltpu.HBM)
        return pl.pallas_call(
            kernel,
            out_shape=jax.ShapeDtypeStruct(q.shape, q.dtype),
            in_specs=[hbm, hbm, hbm],
            out_specs=pl.BlockSpec(memory_space=pltpu.VMEM),
            scratch_shapes=[
                pltpu.VMEM((kv, ranks * tokens, dim), BF16),
                pltpu.VMEM((kv, ranks * tokens, dim), BF16),
                pltpu.VMEM((kv, rows, dim), BF16),
                pltpu.VMEM((4, kv, rows, 2 * tokens), F32),
                pltpu.VMEM((4, kv, rows, 2 * tokens), BF16),
                pltpu.VMEM((kv, rows, dim), F32),
                pltpu.VMEM((kv, rows, dim), F32),
                pltpu.VMEM((kv, rows, dim), F32),
                pltpu.VMEM((tokens, heads, dim), BF16),
                pltpu.VMEM((tokens, kv, dim), BF16),
                pltpu.VMEM((tokens, kv, dim), BF16),
                pltpu.VMEM((tokens * heads, dim), F32),
                pltpu.SemaphoreType.DMA((3,)),
                pltpu.SemaphoreType.DMA((72,)),
                pltpu.SemaphoreType.DMA((7 * NU,)),
            ],
            compiler_params=pltpu.CompilerParams(collective_id=0, has_side_effects=True, vmem_limit_bytes=54 * 2**20),
        )(q, k, v)

    return jax.shard_map(local, mesh=mesh, in_specs=(seq_spec, seq_spec, seq_spec), out_specs=seq_spec, check_vma=False)
```

time: 45.7 us -> 32.9 us (0.72)
  Pallas kernels: 43.1 us -> 30.3 us
    pallas_call x1, Pallas kernels: 43.1 us -> 30.3 us  [local(): pl.pallas_call(kernel, out_shape=jax.ShapeDtypeStruct(q.shape, q.dtype),...]
where the time goes in v2:
time: 32.9 us; the launch traced here: 32.8 us
  Pallas kernels  30.3 us (92%)
  local copies, waits for them, and re-layouts  2.49 us (8%)
    pallas_call x1, Pallas kernels, local(): pl.pallas_call(kernel, out_shape=jax.ShapeDtypeStruct(q.shape, q.dtype),...  30.3 us
    unnamed x1, local copies, waits for them, and re-layouts  2.49 us

profile of v2, /device:TPU:7, one launch (start us, length us, event | category | flops | bytes accessed | tf_op | source)
XLA Modules:
  0.0 32.8 jit_solution(689369914933233871)
XLA Ops:
  0.0 30.3 %shard_map.37 = bf16[128,40,128]{2,1,0:T(8,128)(2,1)} custom-call(bf16[128,40,128]{2,1,0:T(8,128)(2,1)} %q_hbm.1, bf16[128,8,128]{2,1,0:T(8,128)(2,1)} %k_hbm.1, bf16[128,8,128]{2,1,0:T(8,128)(2,1)} %v_hbm.1), custom_call_target="tpu_custom_call" | custom-call | tf_op jit(solution)/shard_map/pallas_call | solution.py:295
  30.3 2.5 %copy.5 = bf16[128,40,128]{2,1,0:T(8,128)(2,1)} copy(bf16[128,40,128]{2,1,0:T(8,128)(2,1)} %shard_map.37) | data formatting | bytes 2621440

commit v3 on v2

--- a/solution.py
+++ b/solution.py
@@ -44,8 +44,13 @@
     for load in loads:
         load.start()
     barrier = pltpu.get_barrier_semaphore()
-    for dev in (dev_x, dev_y, dev_p):
-        pl.semaphore_signal(barrier, inc=1, device_id=dev, device_id_type=MESH)
+    pl.semaphore_signal(barrier, inc=1, device_id=dev_p, device_id_type=MESH)
+    pl.semaphore_signal(barrier, inc=1, device_id=dev_x, device_id_type=MESH)
+
+    @pl.when(iy == 1)
+    def _():
+        pl.semaphore_signal(barrier, inc=1, device_id=dev_y, device_id_type=MESH)
+
 
     def split_heads(raw, heads, put):
         step = 32
@@ -70,31 +75,58 @@
     def put_q(h, val):
         qt[h // group, pl.ds((h % group) * tokens, tokens), :] = val
 
+    top, low, right, left = iy == 1, iy == 0, ix == 1, ix == 0
+    not_third, not_last = chip != 2, chip != 3
     sends = []
+
+    def when(cond, body):
+        body() if cond is None else pl.when(cond)(body)
 
     def piece(unit, src):
         h0, n, _ = UNITS[unit]
         buf = kbuf if unit < NK else vbuf
         return buf.at[pl.ds(h0, n), pl.ds(pl.multiple_of(rank_of[src] * tokens, tokens), tokens), :]
 
-    def send(unit, src, dev, as_src):
-        ref = piece(unit, src)
-        copy = pltpu.make_async_remote_copy(ref, ref, ssem.at[len(sends)], rsem.at[as_src * NU + unit], device_id=dev, device_id_type=MESH)
-        copy.start()
-        sends.append(copy)
-
-    def arrive(unit, src):
-        ref = piece(unit, src)
-        pltpu.make_async_remote_copy(ref, ref, ssem.at[0], rsem.at[src * NU + unit], device_id=dev_p, device_id_type=MESH).wait_recv()
-
-    def own_link(unit, which):
-        send(unit, ME, (dev_x, dev_y)[which], (X, Y)[which])
-
-    def share(unit, src):
-        send(unit, src, dev_p, {X: PX, Y: PY, Z: PZ}[src])
-
-    def relay(unit, src):
-        send(unit, src, {X: dev_y, Y: dev_x}[src], Z)
+    def send(cond, moves):
+        first = len(sends)
+        for i, (unit, src, dev, as_src) in enumerate(moves):
+            ref = piece(unit, src)
+            sends.append(pltpu.make_async_remote_copy(ref, ref, ssem.at[first + i], rsem.at[as_src * NU + unit], device_id=dev, device_id_type=MESH))
+        copies = sends[first:]
+        when(cond, lambda: [copy.start() for copy in copies] and None)
+        drains.append((cond, copies))
+
+    drains = []
+
+    def arrive(cond, units, srcs):
+        def body():
+            for unit in units:
+                for src in srcs:
+                    ref = piece(unit, src)
+                    pltpu.make_async_remote_copy(ref, ref, ssem.at[0], rsem.at[src * NU + unit], device_id=dev_p, device_id_type=MESH).wait_recv()
+
+        when(cond, body)
+
+    def path(unit):
+        return UNITS[unit][2]
+
+    def own_x(unit):
+        send(left if path(unit) else not_last, [(unit, ME, dev_x, X)])
+
+    def own_y(unit):
+        send(low, [(unit, ME, dev_y, Y)])
+
+    def own_partner(units):
+        send(None, [(unit, ME, dev_p, PT) for unit in units])
+
+    def arrive_x(unit):
+        arrive(right if path(unit) else not_third, [unit], [X])
+
+    def share(units, src):
+        send(right if src == X else top, [(unit, src, dev_p, {X: PX, Y: PY, Z: PZ}[src]) for unit in units])
+
+    def relay(units, src):
+        send({X: low, Y: top}[src], [(unit, src, {X: dev_y, Y: dev_x}[src], Z) for unit in units])
 
     def by_role(body):
         for role, blocks in enumerate(ROLE_BLOCKS):
@@ -131,53 +163,49 @@
 
     loads[0].wait()
     split_heads(k_raw, num_kv, put_k)
-    pl.semaphore_wait(barrier, 3)
-    own_link(0, 0)
-    own_link(1, 1)
-    own_link(1, 0)
-    own_link(0, 1)
-    for u in range(NK):
-        send(u, ME, dev_p, PT)
+    pl.when(low)(lambda: pl.semaphore_wait(barrier, 3))
+    pl.when(top)(lambda: pl.semaphore_wait(barrier, 2))
+    own_x(0)
+    own_y(1)
+    own_x(1)
+    own_y(0)
+    own_partner(range(NK))
     loads[1].wait()
     split_heads(v_raw, num_kv, put_v)
     loads[2].wait()
     split_heads(q_raw, num_heads, put_q)
-    for u in range(NK):
-        arrive(u, PT)
+    arrive(None, range(NK), [PT])
     for h in range(num_kv):
         score_own(h)
 
-    arrive(0, X)
-    relay(0, X)
-    arrive(1, Y)
-    relay(1, Y)
-    share(0, X)
-    share(1, Y)
+    arrive_x(0)
+    relay([0], X)
+    arrive(top, [1], [Y])
+    relay([1], Y)
+    share([0], X)
+    share([1], Y)
     for a, b in ((0, 1), (1, 0), (2, 3), (3, 2)):
-        own_link(NK + a, 0)
-        own_link(NK + b, 1)
-    for u in range(NV):
-        send(NK + u, ME, dev_p, PT)
-    arrive(0, PX)
+        own_x(NK + a)
+        own_y(NK + b)
+    own_partner(range(NK, NK + NV))
+    arrive(right, [0], [PX])
     scores_of(X, 0)
-    arrive(1, PY)
+    arrive(top, [1], [PY])
     scores_of(Y, 1)
-    arrive(1, X)
-    share(1, X)
-    arrive(0, Y)
-    share(0, Y)
-    arrive(1, PX)
+    arrive_x(1)
+    share([1], X)
+    arrive(top, [0], [Y])
+    share([0], Y)
+    arrive(right, [1], [PX])
     scores_of(X, 1)
-    arrive(0, PY)
+    arrive(top, [0], [PY])
     scores_of(Y, 0)
-    arrive(0, Z)
-    share(0, Z)
-    arrive(1, Z)
-    share(1, Z)
-    arrive(0, PZ)
-    scores_of(Z, 0)
-    arrive(1, PZ)
-    scores_of(Z, 1)
+    for u in range(NK):
+        arrive(top, [u], [Z])
+        share([u], Z)
+    for u in range(NK):
+        arrive(top, [u], [PZ])
+        scores_of(Z, u)
 
     log2_scale = dim ** -0.5 * math.log2(math.e)
     step_rows = 64
@@ -218,17 +246,21 @@
             f_buf[pl.ds(h * group + n, tokens, stride=num_heads), :] = out[n * tokens : (n + 1) * tokens, :]
 
     def values_from_links(u):
-        arrive(NK + u, X)
-        arrive(NK + u, Y)
-        h0, n, path = V_UNITS[u]
-        for h in range(h0, h0 + n):
-            relay(NK + NV + h, (X, Y)[path])
-        share(NK + u, X)
-        share(NK + u, Y)
+        h0, n, way = V_UNITS[u]
+        second = [NK + NV + h for h in range(h0, h0 + n)]
+        arrive_x(NK + u)
+        if way == 0:
+            relay(second, X)
+        share([NK + u], X)
+        arrive(top, [NK + u], [Y])
+        if way == 1:
+            relay(second, Y)
+        share([NK + u], Y)
 
     def values_from_partner(u):
-        for src in (PT, PX, PY):
-            arrive(NK + u, src)
+        arrive(None, [NK + u], [PT])
+        arrive(right, [NK + u], [PX])
+        arrive(top, [NK + u], [PY])
 
     def stage(h):
         def body(blocks):
@@ -264,13 +296,13 @@
     near_stage(NV - 1)
     order = (0, 2, 1, 3, 4, 6, 5, 7)
     for i, h in enumerate(order):
-        arrive(NK + NV + h, Z)
-        share(NK + NV + h, Z)
+        arrive(top, [NK + NV + h], [Z])
+        share([NK + NV + h], Z)
         if i > 0:
             g = order[i - 1]
-            arrive(NK + NV + g, PZ)
+            arrive(top, [NK + NV + g], [PZ])
             by_role(lambda blocks: last(g, blocks))
-    arrive(NK + NV + order[-1], PZ)
+    arrive(top, [NK + NV + order[-1]], [PZ])
     by_role(lambda blocks: last(order[-1], blocks))
 
     def narrow(i, carry):
@@ -279,8 +311,8 @@
         return carry
 
     lax.fori_loop(0, tokens // 16, narrow, 0)
-    for copy in sends:
-        copy.wait_send()
+    for cond, copies in drains:
+        when(cond, lambda: [copy.wait_send() for copy in copies] and None)
 
 
 def solution(mesh):
@@ -294,7 +326,7 @@
         hbm = pl.BlockSpec(memory_space=pltpu.HBM)
         return pl.pallas_call(
             kernel,
-            out_shape=jax.ShapeDtypeStruct(q.shape, q.dtype),
+            out_shape=pltpu.VMEM(q.shape, q.dtype),
             in_specs=[hbm, hbm, hbm],
             out_specs=pl.BlockSpec(memory_space=pltpu.VMEM),
             scratch_shapes=[
@@ -315,6 +347,6 @@
                 pltpu.SemaphoreType.DMA((7 * NU,)),
             ],
             compiler_params=pltpu.CompilerParams(collective_id=0, has_side_effects=True, vmem_limit_bytes=54 * 2**20),
-        )(q, k, v)
+        )(*[pltpu.with_memory_space_constraint(a, pltpu.HBM) for a in (q, k, v)])
 
     return jax.shard_map(local, mesh=mesh, in_specs=(seq_spec, seq_spec, seq_spec), out_specs=seq_spec, check_vma=False)

time: 32.9 us -> 30.4 us (0.924)
  local copies, waits for them, and re-layouts: 2.49 us -> 1.06 us
  Pallas kernels: 30.3 us -> 29.2 us
    unnamed x1, local copies, waits for them, and re-layouts: 2.49 us -> 1.06 us
    pallas_call x1, Pallas kernels: 30.3 us -> 29.2 us  [local(): pl.pallas_call(kernel, out_shape=pltpu.VMEM(q.shape, q.dtype), in_specs=[...]
where the time goes in v3:
time: 30.4 us; the launch traced here: 30.3 us
  Pallas kernels  29.2 us (96%)
  local copies, waits for them, and re-layouts  1.06 us (3%)
    pallas_call x1, Pallas kernels, local(): pl.pallas_call(kernel, out_shape=pltpu.VMEM(q.shape, q.dtype), in_specs=[...  29.2 us
    unnamed x1, local copies, waits for them, and re-layouts  1.06 us

profile of v3, /device:TPU:7, one launch (start us, length us, event | category | flops | bytes accessed | tf_op | source)
XLA Modules:
  0.0 30.3 jit_solution(3151154151586834614)
XLA Ops:
  0.0 29.2 %shard_map.37 = bf16[128,40,128]{2,1,0:T(8,128)(2,1)S(1)} custom-call(bf16[128,40,128]{2,1,0:T(8,128)(2,1)} %q_hbm.1, bf16[128,8,128]{2,1,0:T(8,128)(2,1)} %k_hbm.1, bf16[128,8,128]{2,1,0:T(8,128)(2,1)} %v_hbm.1), custom_call_target="tpu_custom_call" | custom-call | tf_op jit(solution)/shard_map/pallas_call | solution.py:327
  29.2 1.1 %copy.5 = bf16[128,40,128]{2,1,0:T(8,128)(2,1)} copy(bf16[128,40,128]{2,1,0:T(8,128)(2,1)S(1)} %shard_map.37) | data formatting | bytes 2621440

commit v4 on v3

--- a/solution.py
+++ b/solution.py
@@ -23,7 +23,7 @@
 ROLE_BLOCKS = ((OWN,), (OWN, X), (OWN, Y, Z), (OWN, X, Y, Z))
 
 
-def kernel(q_hbm, k_hbm, v_hbm, o_ref, kbuf, vbuf, qt, s_buf, p_buf, mp, lsum, acc, q_raw, k_raw, v_raw, f_buf, lsem, ssem, rsem):
+def kernel(q_hbm, k_hbm, v_hbm, o_ref, kbuf, vbuf, qt, s_buf, p_buf, mp, mz, lsum, acc, q_raw, k_raw, v_raw, f_buf, lsem, ssem, rsem):
     tokens, num_heads, dim = q_hbm.shape
     num_kv = k_hbm.shape[1]
     group = num_heads // num_kv
@@ -116,6 +116,17 @@
     def own_y(unit):
         send(low, [(unit, ME, dev_y, Y)])
 
+    def own_values(first):
+        if first:
+            for u in (0, 2, 1, 3):
+                send(chip == 0, [(NK + u, ME, dev_x, X)])
+            for u in (1, 3):
+                send(chip == 0, [(NK + u, ME, dev_y, Y)])
+            return
+        for a, b in ((1, 1), (3, 3), (0, 0), (2, 2)):
+            send(chip == 2 if path(NK + a) else (chip + 1) // 2 == 1, [(NK + a, ME, dev_x, X)])
+            send(chip == 1 if path(NK + b) else low, [(NK + b, ME, dev_y, Y)])
+
     def own_partner(units):
         send(None, [(unit, ME, dev_p, PT) for unit in units])
 
@@ -151,7 +162,7 @@
         s_buf[blk, h] = s
         mp[h] = jnp.maximum(mp[h], jnp.maximum(s[:, :tokens], s[:, tokens:]))
 
-    needed = {X: ix == 1, Y: iy == 1, Z: iy == 1}
+    needed = {X: ix == 1, Y: iy == 1}
 
     def scores_of(blk, unit):
         h0, n, _ = K_UNITS[unit]
@@ -172,6 +183,7 @@
     own_partner(range(NK))
     loads[1].wait()
     split_heads(v_raw, num_kv, put_v)
+    own_values(True)
     loads[2].wait()
     split_heads(q_raw, num_heads, put_q)
     arrive(None, range(NK), [PT])
@@ -184,9 +196,7 @@
     relay([1], Y)
     share([0], X)
     share([1], Y)
-    for a, b in ((0, 1), (1, 0), (2, 3), (3, 2)):
-        own_x(NK + a)
-        own_y(NK + b)
+    own_values(False)
     own_partner(range(NK, NK + NV))
     arrive(right, [0], [PX])
     scores_of(X, 0)
@@ -200,13 +210,6 @@
     scores_of(X, 1)
     arrive(top, [0], [PY])
     scores_of(Y, 0)
-    for u in range(NK):
-        arrive(top, [u], [Z])
-        share([u], Z)
-    for u in range(NK):
-        arrive(top, [u], [PZ])
-        scores_of(Z, u)
-
     log2_scale = dim ** -0.5 * math.log2(math.e)
     step_rows = 64
 
@@ -228,6 +231,25 @@
     def row_sum(h):
         lsum[h] = jnp.broadcast_to(1.0 / jnp.sum(lsum[h], axis=-1, keepdims=True), (rows, dim))
 
+    def far_scores(h):
+        s = scores(Z, h)
+        s_buf[Z, h] = s
+        mz[h] = jnp.maximum(s[:, :tokens], s[:, tokens:])
+
+    def far_probs(h):
+        for r0 in range(0, rows, step_rows):
+            r = pl.ds(r0, step_rows)
+            old = mp[h, r, :]
+            m = jnp.maximum(old, jnp.broadcast_to(jnp.max(mz[h, r, :], axis=-1, keepdims=True) * log2_scale, (step_rows, tokens)))
+            factor = jnp.exp2(old - m)
+            mp[h, r, :] = factor
+            total = lsum[h, r, :] * factor
+            for c0 in (0, tokens):
+                p = jnp.exp2(s_buf[Z, h, r, pl.ds(c0, tokens)] * log2_scale - m)
+                p_buf[Z, h, r, pl.ds(c0, tokens)] = p.astype(BF16)
+                total = total + p
+            lsum[h, r, :] = total
+
     def weighted(h, blocks):
         total = None
         for blk in blocks:
@@ -240,7 +262,7 @@
         acc[h] = weighted(h, [blk for blk in blocks if blk != Z])
 
     def last(h, blocks):
-        out = acc[h] if Z not in blocks else acc[h] + weighted(h, [Z])
+        out = acc[h] if Z not in blocks else acc[h] * mp[h] + weighted(h, [Z])
         out = out * lsum[h]
         for n in range(group):
             f_buf[pl.ds(h * group + n, tokens, stride=num_heads), :] = out[n * tokens : (n + 1) * tokens, :]
@@ -248,30 +270,57 @@
     def values_from_links(u):
         h0, n, way = V_UNITS[u]
         second = [NK + NV + h for h in range(h0, h0 + n)]
+        arrive(top, [NK + u], [Y])
+        if way == 1:
+            relay(second, Y)
+        share([NK + u], Y)
         arrive_x(NK + u)
         if way == 0:
             relay(second, X)
         share([NK + u], X)
-        arrive(top, [NK + u], [Y])
-        if way == 1:
-            relay(second, Y)
-        share([NK + u], Y)
 
     def values_from_partner(u):
         arrive(None, [NK + u], [PT])
         arrive(right, [NK + u], [PX])
         arrive(top, [NK + u], [PY])
 
-    def stage(h):
+    def stage(heads):
         def body(blocks):
-            if h == 0:
-                row_max(0)
-            if h + 1 < num_kv:
-                row_max(h + 1)
-            if h < num_kv:
-                probs(h, blocks)
-            if h > 0:
-                row_sum(h - 1)
+            for h in heads:
+                if h == 0:
+                    row_max(0)
+                if h + 1 < num_kv:
+                    row_max(h + 1)
+                probs(h, [blk for blk in blocks if blk != Z])
+
+        by_role(body)
+
+    def far_stage(heads):
+        def body(blocks):
+            for h in heads:
+                if Z in blocks:
+                    if h == 0:
+                        far_scores(0)
+                    if h + 1 < num_kv:
+                        far_scores(h + 1)
+                    if h < num_kv:
+                        far_probs(h)
+                if h > 0:
+                    row_sum(h - 1)
+
+        by_role(body)
+
+    def second_hop(heads):
+        for h in heads:
+            arrive(top, [NK + NV + h], [Z])
+            share([NK + NV + h], Z)
+
+    def last_stage(heads):
+        arrive(top, [NK + NV + h for h in heads], [PZ])
+
+        def body(blocks):
+            for h in heads:
+                last(h, blocks)
 
         by_role(body)
 
@@ -284,26 +333,31 @@
 
         by_role(body)
 
-    for u in range(NV):
-        stage(2 * u)
+    stage((0, 1))
+    for u in range(NK):
+        arrive(top, [u], [Z])
+        share([u], Z)
+    stage((2, 3))
+    stage((4, 5))
+    stage((6, 7))
+    arrive(top, range(NK), [PZ])
+    turn = (1, 3, 0, 2)
+    for i, u in enumerate(turn):
         values_from_links(u)
-        stage(2 * u + 1)
-        if u > 0:
-            values_from_partner(u - 1)
-            near_stage(u - 1)
-    stage(num_kv)
-    values_from_partner(NV - 1)
-    near_stage(NV - 1)
-    order = (0, 2, 1, 3, 4, 6, 5, 7)
-    for i, h in enumerate(order):
-        arrive(top, [NK + NV + h], [Z])
-        share([NK + NV + h], Z)
+        far_stage((2 * i, 2 * i + 1) if i < NV - 1 else (2 * i, 2 * i + 1, num_kv))
         if i > 0:
-            g = order[i - 1]
-            arrive(top, [NK + NV + g], [PZ])
-            by_role(lambda blocks: last(g, blocks))
-    arrive(top, [NK + NV + order[-1]], [PZ])
-    by_role(lambda blocks: last(order[-1], blocks))
+            values_from_partner(turn[i - 1])
+            near_stage(turn[i - 1])
+    second_hop((0, 2))
+    second_hop((1, 3))
+    values_from_partner(turn[-1])
+    near_stage(turn[-1])
+    second_hop((4, 6))
+    last_stage((0, 2))
+    second_hop((5, 7))
+    last_stage((1, 3))
+    last_stage((4, 6))
+    last_stage((5, 7))
 
     def narrow(i, carry):
         t = pl.multiple_of(i * 16, 16)
@@ -338,15 +392,16 @@
                 pltpu.VMEM((kv, rows, dim), F32),
                 pltpu.VMEM((kv, rows, dim), F32),
                 pltpu.VMEM((kv, rows, dim), F32),
+                pltpu.VMEM((kv, rows, dim), F32),
                 pltpu.VMEM((tokens, heads, dim), BF16),
                 pltpu.VMEM((tokens, kv, dim), BF16),
                 pltpu.VMEM((tokens, kv, dim), BF16),
                 pltpu.VMEM((tokens * heads, dim), F32),
                 pltpu.SemaphoreType.DMA((3,)),
-                pltpu.SemaphoreType.DMA((72,)),
+                pltpu.SemaphoreType.DMA((80,)),
                 pltpu.SemaphoreType.DMA((7 * NU,)),
             ],
-            compiler_params=pltpu.CompilerParams(collective_id=0, has_side_effects=True, vmem_limit_bytes=54 * 2**20),
+            compiler_params=pltpu.CompilerParams(collective_id=0, has_side_effects=True, vmem_limit_bytes=57 * 2**20),
         )(*[pltpu.with_memory_space_constraint(a, pltpu.HBM) for a in (q, k, v)])
 
     return jax.shard_map(local, mesh=mesh, in_specs=(seq_spec, seq_spec, seq_spec), out_specs=seq_spec, check_vma=False)

time: 30.4 us -> 26.5 us (0.87)
  the two profiles are of different devices: /device:TPU:7 before, /device:TPU:5 now
where the time goes in v4:
time: 26.5 us; the launch traced here: 26.4 us
  Pallas kernels  25.4 us (96%)
  local copies, waits for them, and re-layouts  1.06 us (4%)
    pallas_call x1, Pallas kernels, local(): pl.pallas_call(kernel, out_shape=pltpu.VMEM(q.shape, q.dtype), in_specs=[...  25.4 us
    unnamed x1, local copies, waits for them, and re-layouts  1.06 us

profile of v4, /device:TPU:5, one launch (start us, length us, event | category | flops | bytes accessed | tf_op | source)
XLA Modules:
  0.0 26.4 jit_solution(16853510284531561959)
XLA Ops:
  0.0 25.4 %shard_map.37 = bf16[128,40,128]{2,1,0:T(8,128)(2,1)S(1)} custom-call(bf16[128,40,128]{2,1,0:T(8,128)(2,1)} %q_hbm.1, bf16[128,8,128]{2,1,0:T(8,128)(2,1)} %k_hbm.1, bf16[128,8,128]{2,1,0:T(8,128)(2,1)} %v_hbm.1), custom_call_target="tpu_custom_call" | custom-call | tf_op jit(solution)/shard_map/pallas_call | solution.py:381
  25.4 1.1 %copy.5 = bf16[128,40,128]{2,1,0:T(8,128)(2,1)} copy(bf16[128,40,128]{2,1,0:T(8,128)(2,1)S(1)} %shard_map.37) | data formatting | bytes 2621440

commit v5 on v4

--- a/solution.py
+++ b/solution.py
@@ -120,12 +120,11 @@
         if first:
             for u in (0, 2, 1, 3):
                 send(chip == 0, [(NK + u, ME, dev_x, X)])
-            for u in (1, 3):
-                send(chip == 0, [(NK + u, ME, dev_y, Y)])
+            send(chip == 0, [(NK + 1, ME, dev_y, Y)])
             return
         for a, b in ((1, 1), (3, 3), (0, 0), (2, 2)):
             send(chip == 2 if path(NK + a) else (chip + 1) // 2 == 1, [(NK + a, ME, dev_x, X)])
-            send(chip == 1 if path(NK + b) else low, [(NK + b, ME, dev_y, Y)])
+            send(chip == 1 if b == 1 else low, [(NK + b, ME, dev_y, Y)])
 
     def own_partner(units):
         send(None, [(unit, ME, dev_p, PT) for unit in units])

time: 26.5 us -> 25.1 us (0.947)
  the two profiles are of different devices: /device:TPU:5 before, /device:TPU:7 now
where the time goes in v5:
time: 25.1 us; the launch traced here: 24.9 us
  Pallas kernels  23.8 us (95%)
  local copies, waits for them, and re-layouts  1.06 us (4%)
    pallas_call x1, Pallas kernels, local(): pl.pallas_call(kernel, out_shape=pltpu.VMEM(q.shape, q.dtype), in_specs=[...  23.8 us
    unnamed x1, local copies, waits for them, and re-layouts  1.06 us

profile of v5, /device:TPU:7, one launch (start us, length us, event | category | flops | bytes accessed | tf_op | source)
XLA Modules:
  0.0 24.9 jit_solution(4339014596596899989)
XLA Ops:
  0.0 23.8 %shard_map.37 = bf16[128,40,128]{2,1,0:T(8,128)(2,1)S(1)} custom-call(bf16[128,40,128]{2,1,0:T(8,128)(2,1)} %q_hbm.1, bf16[128,8,128]{2,1,0:T(8,128)(2,1)} %k_hbm.1, bf16[128,8,128]{2,1,0:T(8,128)(2,1)} %v_hbm.1), custom_call_target="tpu_custom_call" | custom-call | tf_op jit(solution)/shard_map/pallas_call | solution.py:380
  23.8 1.1 %copy.5 = bf16[128,40,128]{2,1,0:T(8,128)(2,1)} copy(bf16[128,40,128]{2,1,0:T(8,128)(2,1)S(1)} %shard_map.37) | data formatting | bytes 2621440

commit v6 on v5

--- a/solution.py
+++ b/solution.py
@@ -120,11 +120,10 @@
         if first:
             for u in (0, 2, 1, 3):
                 send(chip == 0, [(NK + u, ME, dev_x, X)])
-            send(chip == 0, [(NK + 1, ME, dev_y, Y)])
             return
         for a, b in ((1, 1), (3, 3), (0, 0), (2, 2)):
             send(chip == 2 if path(NK + a) else (chip + 1) // 2 == 1, [(NK + a, ME, dev_x, X)])
-            send(chip == 1 if b == 1 else low, [(NK + b, ME, dev_y, Y)])
+            send(low, [(NK + b, ME, dev_y, Y)])
 
     def own_partner(units):
         send(None, [(unit, ME, dev_p, PT) for unit in units])
@@ -350,11 +349,10 @@
     second_hop((0, 2))
     second_hop((1, 3))
     values_from_partner(turn[-1])
+    second_hop((4, 6))
     near_stage(turn[-1])
-    second_hop((4, 6))
-    last_stage((0, 2))
     second_hop((5, 7))
-    last_stage((1, 3))
+    last_stage((0, 2, 1, 3))
     last_stage((4, 6))
     last_stage((5, 7))
 

time: 25.1 us -> 24.7 us (0.984)
  Pallas kernels: 23.8 us -> 23.5 us
    pallas_call x1, Pallas kernels: 23.8 us -> 23.5 us  [local(): pl.pallas_call(kernel, out_shape=pltpu.VMEM(q.shape, q.dtype), in_specs=[...]
where the time goes in v6:
time: 24.7 us; the launch traced here: 24.6 us
  Pallas kernels  23.5 us (95%)
  local copies, waits for them, and re-layouts  1.06 us (4%)
    pallas_call x1, Pallas kernels, local(): pl.pallas_call(kernel, out_shape=pltpu.VMEM(q.shape, q.dtype), in_specs=[...  23.5 us
    unnamed x1, local copies, waits for them, and re-layouts  1.06 us

profile of v6, /device:TPU:7, one launch (start us, length us, event | category | flops | bytes accessed | tf_op | source)
XLA Modules:
  0.0 24.6 jit_solution(15773224251301262399)
XLA Ops:
  0.0 23.5 %shard_map.37 = bf16[128,40,128]{2,1,0:T(8,128)(2,1)S(1)} custom-call(bf16[128,40,128]{2,1,0:T(8,128)(2,1)} %q_hbm.1, bf16[128,8,128]{2,1,0:T(8,128)(2,1)} %k_hbm.1, bf16[128,8,128]{2,1,0:T(8,128)(2,1)} %v_hbm.1), custom_call_target="tpu_custom_call" | custom-call | tf_op jit(solution)/shard_map/pallas_call | solution.py:378
  23.5 1.1 %copy.5 = bf16[128,40,128]{2,1,0:T(8,128)(2,1)} copy(bf16[128,40,128]{2,1,0:T(8,128)(2,1)S(1)} %shard_map.37) | data formatting | bytes 2621440
